TPU v7x, 32 devices: a whole 2x2x4 slice. The times are simulated.
32 devices in a mesh: batch: 2 (over core), token: 8 (over z, x), hidden: 2 (over y).
Axes of the slice: x: 2, y: 2, z: 4, core: 2. Of those that a mesh axis runs over, the one named last changes fastest.
Arguments:
- hist_len: int32 [128], replicated, may hold values from 32 to 512, as said below
- queries: bfloat16 [32, 1536], P(None, 'token'), may hold values from -4 to 4
- history_keys: bfloat16 [384, 1536, 128], P(('batch', 'hidden'), 'token'), may hold values from -192 to 192
- cached_history_values: bfloat16 [384, 1536, 128], P(('batch', 'hidden'), 'token'), may hold values from -6 to 6
- gain_mix: float32 [1536], replicated, may hold values from 0.25 to 1.75
- w_up: bfloat16 [32, 1536, 3072], P('token', None, 'hidden'), may hold values from -0.15625 to 0.15625
- w_down: bfloat16 [32, 3072, 1536], P('token', 'hidden'), may hold values from -0.109375 to 0.109375
- gain_out: float32 [1536], replicated, may hold values from 0.25 to 1.75
Outputs:
- mixer_out: bfloat16 [128, 32, 1536], P(('batch', 'hidden'), 'token')
Inputs may be any that keep to these rules, and one draw needn't show every extreme that they name: `hist_len`: along batch+hidden, the requests of each index need between 32 and 96 slots, indices 2i and 2i + 1 need 4 * 32 slots together, and some index needs exactly 96; within an index, requests 2j and 2j + 1 need from 2 to 6 slots together.
All inputs are finite; a program needn't handle non-finite values.
Results may differ from a plain program's by a relative error of at most 0.015.
Values may be sent and summed in bfloat16 or wider, within the bound.
No kernel may reach another device: no remote copies, remote signals or barrier semaphores. Data moves between devices by JAX's collectives and lax.ppermute only.
A program may use at most 128 MiB of HBM per device.

v0:
```python
import jax
import jax.numpy as jnp
from jax import lax
from jax.sharding import PartitionSpec as P

TOKEN_COUNT = 32
MODEL_WIDTH = 1536
BLOCK_POSITIONS = 128
REQ_DEV = 32
EPSILON = 1e-05
NEGATIVE_FILL = -1e30


def slot_layout(lengths, slot_count, block_rows):
    request_count = lengths.shape[0]
    blocks = (lengths + block_rows - 1) // block_rows
    block_ends = jnp.cumsum(blocks)
    block_starts = block_ends - blocks
    slot_index = jnp.arange(slot_count, dtype=jnp.int32)
    owners = jnp.sum((block_ends[None, :] <= slot_index[:, None]).astype(jnp.int32), axis=1)
    onehot = owners[:, None] == jnp.arange(request_count, dtype=jnp.int32)[None, :]
    start_of = jnp.sum(jnp.where(onehot, block_starts[None, :], 0), axis=1)
    length_of = jnp.sum(jnp.where(onehot, lengths[None, :], 0), axis=1)
    valid_rows = jnp.clip(length_of - (slot_index - start_of) * block_rows, 0, block_rows)
    return (onehot, valid_rows)


def block_partials(query_heads, slot_keys, slot_values, valid_rows, score_scale):
    scores = (
        jnp.einsum("qhs,nhsp->nqhp", query_heads, slot_keys, preferred_element_type=jnp.float32)
        * score_scale
    )
    position = jnp.arange(slot_keys.shape[-1], dtype=jnp.int32)
    in_range = position[None, None, None, :] < valid_rows[:, None, None, None]
    scores = jnp.where(in_range, scores, NEGATIVE_FILL)
    maxima = jnp.max(scores, axis=-1)
    softmax_terms = jnp.where(in_range, jnp.exp(scores - maxima[..., None]), 0.0)
    totals = jnp.sum(softmax_terms, axis=-1)
    weighted = jnp.einsum(
        "nqhp,nhsp->nqhs",
        softmax_terms.astype(jnp.bfloat16),
        slot_values,
        preferred_element_type=jnp.float32,
    )
    return (maxima, totals, weighted)


def combine_blocks(maxima, totals, weighted, onehot):
    owned = onehot.astype(jnp.float32)
    is_live = jnp.sum(owned, axis=1) > 0.5
    masked_max = jnp.where(onehot[:, :, None, None], maxima[:, None, :, :], NEGATIVE_FILL)
    request_max = jnp.max(masked_max, axis=0)
    owner_max = jnp.einsum("nr,rqh->nqh", owned, request_max, precision=lax.Precision.HIGHEST)
    factor = jnp.exp(jnp.where(is_live[:, None, None], maxima - owner_max, NEGATIVE_FILL))
    denominator = jnp.einsum("nr,nqh->rqh", owned, factor * totals, precision=lax.Precision.HIGHEST)
    numerator = jnp.einsum(
        "nr,nqhs->rqhs", owned, factor[..., None] * weighted, precision=lax.Precision.HIGHEST
    )
    return (numerator / denominator[..., None]).astype(jnp.bfloat16)


def layer_norm(summand):
    average = jnp.mean(summand, axis=-1, keepdims=True)
    centred = summand - average
    variance = jnp.mean(centred * centred, axis=-1, keepdims=True)
    return centred * lax.rsqrt(variance + EPSILON)


def local(hist_len, queries, history_keys, cached_history_values, gain_mix, w_up, w_down, gain_out):
    group_size = lax.axis_size(("batch", "hidden"))
    my_index = lax.axis_index(("batch", "hidden"))
    head_size = MODEL_WIDTH // TOKEN_COUNT
    local_heads = history_keys.shape[1] // head_size
    slot_count = history_keys.shape[0]
    score_scale = head_size ** (-0.5)
    query_heads = queries.reshape(TOKEN_COUNT, local_heads, head_size)
    all_lengths = hist_len.reshape(group_size, REQ_DEV)
    peer_ids = jnp.arange(group_size, dtype=jnp.int32)
    mine_hot = peer_ids == my_index
    own_lengths = jnp.sum(jnp.where(mine_hot[:, None], all_lengths, 0), axis=0)
    onehot, valid_rows = slot_layout(own_lengths, slot_count, BLOCK_POSITIONS)
    slot_keys = history_keys.reshape(slot_count, local_heads, head_size, BLOCK_POSITIONS)
    slot_values = cached_history_values.reshape(slot_count, local_heads, head_size, BLOCK_POSITIONS)
    maxima, totals, weighted = block_partials(
        query_heads, slot_keys, slot_values, valid_rows, score_scale
    )
    attended = combine_blocks(maxima, totals, weighted, onehot)
    unmixed = lax.all_to_all(
        attended.reshape(REQ_DEV, TOKEN_COUNT, local_heads * head_size),
        "token",
        split_axis=1,
        concat_axis=2,
        tiled=True,
    )
    mixed_rows = jnp.transpose(attended, (0, 2, 1, 3)).reshape(
        REQ_DEV, local_heads, TOKEN_COUNT * head_size
    )
    joined = mixed_rows.astype(jnp.float32) + unmixed.astype(jnp.float32)
    normed = (layer_norm(joined) * gain_mix).astype(jnp.bfloat16)
    lifted = jnp.einsum(
        "ntd,tdf->ntf",
        lax.all_gather(normed, "hidden", axis=0, tiled=True),
        w_up,
        preferred_element_type=jnp.float32,
    )
    activated = jax.nn.gelu(lifted, approximate=False).astype(jnp.bfloat16)
    partial_sums = jnp.einsum("ntf,tfd->ntd", activated, w_down, preferred_element_type=jnp.float32)
    summed = lax.psum_scatter(partial_sums, "hidden", scatter_dimension=0, tiled=True)
    return (layer_norm(summed + normed.astype(jnp.float32)) * gain_out).astype(jnp.bfloat16)


def solution(mesh):
    return jax.shard_map(
        local,
        mesh=mesh,
        in_specs=(
            P(),
            P(None, "token"),
            P(("batch", "hidden"), "token", None),
            P(("batch", "hidden"), "token", None),
            P(),
            P("token", None, "hidden"),
            P("token", "hidden", None),
            P(),
        ),
        out_specs=P(("batch", "hidden"), "token", None),
        check_vma=False,
    )
```

profile of v0, /device:TPU:0, one launch (start us, length us, event | category | flops | bytes accessed | tf_op | source)
XLA Modules:
  0.0 143.5 jit_solution(5583828405777841937)
XLA Ops:
  6.5 0.7 reshape.210
  7.3 0.1 select_reduce_fusion.3
  7.4 0.1 copy.54
  7.5 0.1 reduce-window.7
  7.5 0.1 reduce.2
  7.6 0.1 convert_reduce_fusion.1
  7.8 0.1 select_reduce_fusion.1
  7.9 0.5 broadcast_compare_fusion
  8.4 0.0 copy-done.2
  8.4 0.1 iota_compare_fusion
  8.5 0.8 reshape.213
  9.3 6.7 %bitcast_reduce_fusion = (f32[96,32,4]{1,0,2:T(8,128)S(1)}, f32[4,96,128,32]{2,3,1,0:T(8,128)}) fusion(pred[96,128]{1,0:T(8,128)(4,1)S(1)} %iota_compare_fusion, bf16[96,4,48,128]{3,2,1,0:T(8,128)(2,1)} %bitcast.131, bf16[32,4,48,1]{2,1,0,3:T(4,128)(2,1)S(1)} %bitcast.134), kind=kOutput, calls=%fused_computation.2 | convolution fusion | flops 155701248 | bytes 11083776 | tf_op jit(solution)/shard_map/qhs,nhsp->nqhp/dot_general | solution.py:30
  16.1 0.7 copy.59
  16.8 6.0 %fusion.6 = (f32[96,32,4]{1,0,2:T(8,128)S(1)}, bf16[96,32,4,128]{3,1,0,2:T(8,128)(2,1)S(1)}) fusion(f32[4,96,128,32]{2,3,1,0:T(8,128)} %get-tuple-element.12, f32[96,32,4]{1,0,2:T(8,128)S(1)} %get-tuple-element.11, pred[96,128]{1,0:T(8,128)(4,1)S(1)} %iota_compare_fusion), kind=kLoop, calls=%fused_computation.10 | loop fusion | flops 9424896 | bytes 9547776 | tf_op jit(solution)/shard_map/reduce_sum | solution.py:38
  22.8 0.7 copy.63
  23.5 1.5 %select_reduce_fusion = f32[32,32,4]{1,2,0:T(4,128)S(1)} fusion(f32[96,32,4]{0,1,2:T(8,128)} %copy.59, pred[96,32]{0,1:T(8,128)(4,1)S(1)} %iota_compare_fusion.1), kind=kLoop, calls=%fused_computation.21 | loop fusion | flops 782336 | bytes 68608 | tf_op jit(solution)/shard_map/reduce_max | solution.py:52
  25.0 1.1 fusion.32
  26.1 0.1 copy.60
  26.2 1.1 fusion.68
  27.3 0.1 copy.66
  27.4 0.0 copy-start.3
  27.4 4.8 %bitcast_multiply_fusion = f32[96,32,4,48]{3,1,2,0:T(8,128)S(1)} fusion(f32[96,32,4]{1,2,0:T(4,128)S(1)} %copy.60, bf16[96,4,48,128]{3,2,1,0:T(8,128)(2,1)} %bitcast.130, bf16[96,32,4,128]{3,1,0,2:T(8,128)(2,1)S(1)} %get-tuple-element.10), kind=kOutput, calls=%fused_computation | convolution fusion | flops 151584768 | bytes 10272768 | tf_op jit(solution)/shard_map/nqhp,nhsp->nqhs/dot_general | solution.py:39
  32.3 8.8 %divide_convert_fusion = (bf16[32,32,4,48]{3,0,2,1:T(8,128)(2,1)S(1)}, f32[32,32,4,48]{3,0,2,1:T(8,128)}) fusion(f32[32,32,4]{0,2,1:T(4,128)S(1)} %copy.66, f32[96,32,4,48]{3,1,2,0:T(8,128)S(1)} %bitcast_multiply_fusion, s32[96]{0:T(128)S(1)} %copy-done.3), kind=kOutput, calls=%fused_computation.20 | convolution fusion | flops 226888704 | bytes 3555712 | tf_op jit(solution)/shard_map/nr,nqhs->rqhs/dot_general | solution.py:56
  41.1 0.5 copy.77
  41.7 1.4 reshape.224
  43.0 7.3 %all-to-all-start = ((bf16[32,32,192]{2,0,1:T(8,128)(2,1)}), bf16[32,32,192]{2,0,1:T(8,128)(2,1)S(1)}, u32[]{:S(2)}, u32[]{:S(2)}) async-start(bf16[32,32,192]{2,0,1:T(8,128)(2,1)} %reshape.224), calls=%async_computation | async-start | bytes 1048576 | tf_op jit(solution)/shard_map/all_to_all | solution.py:88
  50.3 0.2 reduce-scatter.2.cloned.1.call-start
  50.6 0.1 copy.64
  50.6 14.2 %all-to-all-done = bf16[32,32,192]{2,0,1:T(8,128)(2,1)S(1)} async-done(((bf16[32,32,192]{2,0,1:T(8,128)(2,1)}), bf16[32,32,192]{2,0,1:T(8,128)(2,1)S(1)}, u32[]{:S(2)}, u32[]{:S(2)}) %all-to-all-start) | async-done | bytes 393248 | tf_op jit(solution)/shard_map/all_to_all | solution.py:88
  64.8 0.1 convert_bitcast_fusion
  64.9 0.6 copy.70
  65.6 0.6 copy.69
  66.2 1.3 reshape.217
  67.4 0.5 reshape.218
  67.9 3.9 %fusion.34 = (f32[32,4]{0,1:T(4,128)S(1)}, f32[32,4,32,48]{3,0,1,2:T(8,128)S(1)}) fusion(f32[32,4,32,48]{3,2,1,0:T(8,128)S(1)} %reshape.218, f32[32,4,32]{0,1,2:T(4,128)S(1)} %copy.64, f32[32,32,4,48]{3,0,2,1:T(8,128)} %get-tuple-element.14), kind=kLoop, calls=%fused_computation.50 | loop fusion | flops 982912 | bytes 2376192 | tf_op jit(solution)/shard_map/reduce_sum | solution.py:63
  71.8 2.6 %copy.65 = f32[32,4,32,48]{3,2,0,1:T(8,128)} copy(f32[32,4,32,48]{3,0,1,2:T(8,128)S(1)} %get-tuple-element.8) | data formatting | bytes 1572864 | tf_op jit(solution)/shard_map/convert_element_type | solution.py:98
  74.4 1.4 multiply_reduce_fusion
  75.8 2.9 %reshape.216 = f32[32,4,1536]{2,0,1:T(8,128)S(1)} reshape(f32[32,4,32,48]{3,2,0,1:T(8,128)} %copy.65) | data formatting | bytes 1572864 | tf_op jit(solution)/shard_map/convert_element_type | solution.py:98
  78.8 0.2 multiply_convert_fusion.1
  79.0 10.4 %all_gather.3 = bf16[64,4,1536]{2,0,1:T(8,128)(2,1)S(1)} all-gather(bf16[32,4,1536]{2,0,1:T(8,128)(2,1)S(1)} %multiply_convert_fusion.1), channel_id=1, replica_groups=mesh['batch'=2,'token'=8,'hidden'=2] {'hidden'}, dimensions={0}, use_global_device_ids=true | all-gather | bytes 1179648 | tf_op jit(solution)/shard_map/all_gather | solution.py:102
  89.4 17.5 %convolution_bitcast_fusion = f32[64,4,1536]{2,0,1:T(8,128)} fusion(bf16[4,1536,1536]{2,1,0:T(8,128)(2,1)} %param.14, bf16[64,4,1536]{2,0,1:T(8,128)(2,1)S(1)} %all_gather.3, bf16[4,1536,1536]{2,1,0:T(8,128)(2,1)} %param.13), kind=kOutput, calls=%fused_computation.14 | convolution fusion | flops 2441478144 | bytes 40108032 | tf_op jit(solution)/shard_map/ntf,tfd->ntd/dot_general | solution.py:107
  106.9 0.0 reduce-scatter.2.cloned.1.call-update
  106.9 0.0 copy-start.5
  106.9 26.9 %reduce-scatter.2.cloned.1.call-done = f32[32,4,1536]{2,0,1:T(8,128)} async-done(((f32[64,4,1536]{2,0,1:T(8,128)}), f32[32,4,1536]{2,0,1:T(8,128)}) %reduce-scatter.2.cloned.1.call-update) | async-done | bytes 786448 | tf_op jit(solution)/shard_map/reduce_scatter | solution.py:108
  133.8 1.4 fusion.66
  135.2 0.2 multiply_reduce_fusion.1
  135.4 0.2 multiply_convert_fusion
  135.6 1.1 copy.72
  (19 shorter events, 0.1 us)
Async XLA Ops:
  7.7 0.7 copy-start.2
  27.4 4.9 %copy-start.3 = (s32[96]{0:T(128)S(1)}, s32[96]{0:T(128)}, u32[]{:S(2)}) copy-start(s32[96]{0:T(128)} %copy-done.2) | copy-start | bytes 1156
  43.0 21.8 %all-to-all-start = ((bf16[32,32,192]{2,0,1:T(8,128)(2,1)}), bf16[32,32,192]{2,0,1:T(8,128)(2,1)S(1)}, u32[]{:S(2)}, u32[]{:S(2)}) async-start(bf16[32,32,192]{2,0,1:T(8,128)(2,1)} %reshape.224), calls=%async_computation | async-start | bytes 1048576 | tf_op jit(solution)/shard_map/all_to_all | solution.py:88
  50.3 83.5 %reduce-scatter.2.cloned.1.call-start = ((), (), s32[]{:S(2)}) async-start(), calls=%async_computation.2 | async-start | bytes 2359296 | tf_op jit(solution)/shard_map/reduce_scatter | solution.py:108
  75.8 2.9 %copy-start.1 = (f32[32,4,1536]{2,0,1:T(8,128)S(1)}, f32[32,4,1536]{2,0,1:T(8,128)}, u32[]{:S(2)}) copy-start(f32[32,4,1536]{2,0,1:T(8,128)} %reshape.217) | copy-start | bytes 2359300
  75.8 2.9 %copy-start.4 = (f32[1536]{0:T(1024)S(1)}, f32[1536]{0:T(1024)}, u32[]{:S(2)}) copy-start(f32[1536]{0:T(1024)} %param.12) | copy-start | bytes 18436
  106.9 28.5 %copy-start.5 = (f32[1536]{0:T(1024)S(1)}, f32[1536]{0:T(1024)}, u32[]{:S(2)}) copy-start(f32[1536]{0:T(1024)} %param.15) | copy-start | bytes 18436
  133.8 1.4 copy-start
Sparse Core Ops, SparseCore 0:
  107.0 26.7 reduce-scatter.1
where the time goes:
time: 144 us
  waiting for transfers between devices  41.1 us (29%)
  matrix products  40.1 us (28%)
  other arithmetic  16 us (11%)
  local copies, waits for them, and re-layouts  14.9 us (10%)
  between operations  13.6 us (9%)
  blocking collectives  10.4 us (7%)
  starting transfers between devices  7.5 us (5%)
    reduce_scatter x1, waiting for transfers between devices, local(): lax.psum_scatter(partial_sums, 'hidden', scatter_dimension=0, tiled=True)  26.9 us
    dot_general x1, matrix products, local(): jnp.einsum('ntf,tfd->ntd', activated, w_down, preferred_element_type=jnp....  17.5 us
    all_to_all x1, waiting for transfers between devices, local(): lax.all_to_all(attended.reshape(REQ_DEV, TOKEN_COUNT, local_heads * head_...  14.2 us
    all_gather x1, blocking collectives, local(): lax.all_gather(normed, 'hidden', axis=0, tiled=True)  10.4 us
    dot_general x1, matrix products, combine_blocks(): jnp.einsum('nr,nqhs->rqhs', owned, factor[..., None] * weighted, precisio...  8.84 us
    convert_element_type x6, local copies, waits for them, and re-layouts, local(): joined = mixed_rows.astype(jnp.float32) + unmixed.astype(jnp.float32)  8.46 us
    all_to_all x1, starting transfers between devices, local(): lax.all_to_all(attended.reshape(REQ_DEV, TOKEN_COUNT, local_heads * head_...  7.28 us
    dot_general x1, matrix products, block_partials(): jnp.einsum('qhs,nhsp->nqhp', query_heads, slot_keys, preferred_element_ty...  6.72 us
  transfers between devices with their start and end apart: 2, of which 2 were waited for; matrix products, arithmetic and copies ran while one was open for 0% of the time, Pallas kernels for 0%

commit v1 on v0

--- a/solution.py
+++ b/solution.py
@@ -85,12 +85,20 @@
         query_heads, slot_keys, slot_values, valid_rows, score_scale
     )
     attended = combine_blocks(maxima, totals, weighted, onehot)
-    unmixed = lax.all_to_all(
-        attended.reshape(REQ_DEV, TOKEN_COUNT, local_heads * head_size),
-        "token",
-        split_axis=1,
-        concat_axis=2,
-        tiled=True,
+    unmixed = jnp.concatenate(
+        lax.all_to_all(
+            jnp.stack(
+                jnp.split(
+                    attended.reshape(REQ_DEV, TOKEN_COUNT, local_heads * head_size),
+                    lax.axis_size("token"),
+                    axis=1,
+                )
+            ),
+            "token",
+            0,
+            0,
+        ),
+        axis=2,
     )
     mixed_rows = jnp.transpose(attended, (0, 2, 1, 3)).reshape(
         REQ_DEV, local_heads, TOKEN_COUNT * head_size

time: 144 us -> 149 us (1.035)
  local copies, waits for them, and re-layouts: 14.9 us -> 19.2 us
    unnamed x12 -> x19, local copies, waits for them, and re-layouts: 0.03 us -> 4.55 us
where the time goes in v1:
time: 149 us; the launch traced here: 148 us
  waiting for transfers between devices  41.1 us (28%)
  matrix products  40.1 us (27%)
  local copies, waits for them, and re-layouts  19.2 us (13%)
  other arithmetic  16 us (11%)
  between operations  13.6 us (9%)
  blocking collectives  10.4 us (7%)
  starting transfers between devices  7.5 us (5%)
    reduce_scatter x1, waiting for transfers between devices, local(): lax.psum_scatter(partial_sums, 'hidden', scatter_dimension=0, tiled=True)  26.9 us
    dot_general x1, matrix products, local(): jnp.einsum('ntf,tfd->ntd', activated, w_down, preferred_element_type=jnp....  17.5 us
    all_to_all x1, waiting for transfers between devices, local(): lax.all_to_all(jnp.stack(jnp.split(attended.reshape(REQ_DEV, TOKEN_COUNT,...  14.2 us
    all_gather x1, blocking collectives, local(): lax.all_gather(normed, 'hidden', axis=0, tiled=True)  10.4 us
    dot_general x1, matrix products, combine_blocks(): jnp.einsum('nr,nqhs->rqhs', owned, factor[..., None] * weighted, precisio...  8.84 us
    convert_element_type x6, local copies, waits for them, and re-layouts, local(): joined = mixed_rows.astype(jnp.float32) + unmixed.astype(jnp.float32)  8.46 us
    all_to_all x1, starting transfers between devices, local(): lax.all_to_all(jnp.stack(jnp.split(attended.reshape(REQ_DEV, TOKEN_COUNT,...  7.28 us
    dot_general x1, matrix products, block_partials(): jnp.einsum('qhs,nhsp->nqhp', query_heads, slot_keys, preferred_element_ty...  6.72 us
  transfers between devices with their start and end apart: 2, of which 2 were waited for; matrix products, arithmetic and copies ran while one was open for 0% of the time, Pallas kernels for 0%

profile of v1, /device:TPU:0, one launch (start us, length us, event | category | flops | bytes accessed | tf_op | source)
XLA Modules:
  0.0 147.9 jit_solution(4233486902186870317)
XLA Ops:
  6.5 0.7 reshape.208
  7.3 0.1 select_reduce_fusion.3
  7.4 0.1 copy.63
  7.5 0.1 reduce.2
  7.6 0.1 convert_reduce_fusion.1
  7.8 0.1 select_reduce_fusion.1
  7.9 0.5 broadcast_compare_fusion
  8.5 0.8 reshape.211
  9.3 6.7 %bitcast_reduce_fusion = (f32[96,32,4]{1,0,2:T(8,128)S(1)}, f32[4,96,128,32]{2,3,1,0:T(8,128)}) fusion(pred[96,128]{1,0:T(8,128)(4,1)S(1)} %iota_compare_fusion, bf16[96,4,48,128]{3,2,1,0:T(8,128)(2,1)} %bitcast.159, bf16[32,4,48,1]{2,1,0,3:T(4,128)(2,1)S(1)} %bitcast.161), kind=kOutput, calls=%fused_computation.2 | convolution fusion | flops 155701248 | bytes 11083776 | tf_op jit(solution)/shard_map/qhs,nhsp->nqhp/dot_general | solution.py:30
  16.1 0.7 copy.68
  16.8 6.0 %fusion.6 = (f32[96,32,4]{1,0,2:T(8,128)S(1)}, bf16[96,32,4,128]{3,1,0,2:T(8,128)(2,1)S(1)}) fusion(f32[4,96,128,32]{2,3,1,0:T(8,128)} %get-tuple-element.12, f32[96,32,4]{1,0,2:T(8,128)S(1)} %get-tuple-element.11, pred[96,128]{1,0:T(8,128)(4,1)S(1)} %iota_compare_fusion), kind=kLoop, calls=%fused_computation.10 | loop fusion | flops 9424896 | bytes 9547776 | tf_op jit(solution)/shard_map/reduce_sum | solution.py:38
  22.8 0.7 copy.72
  23.5 1.5 select_reduce_fusion
  25.0 1.1 fusion.32
  26.1 0.1 copy.69
  26.2 1.1 fusion.76
  27.4 4.8 %bitcast_multiply_fusion = f32[96,32,4,48]{3,1,2,0:T(8,128)S(1)} fusion(f32[96,32,4]{1,2,0:T(4,128)S(1)} %copy.69, bf16[96,4,48,128]{3,2,1,0:T(8,128)(2,1)} %bitcast.158, bf16[96,32,4,128]{3,1,0,2:T(8,128)(2,1)S(1)} %get-tuple-element.10), kind=kOutput, calls=%fused_computation | convolution fusion | flops 151584768 | bytes 10272768 | tf_op jit(solution)/shard_map/nqhp,nhsp->nqhs/dot_general | solution.py:39
  32.3 8.8 %divide_convert_fusion = (bf16[32,32,4,48]{3,0,2,1:T(8,128)(2,1)S(1)}, f32[32,32,4,48]{3,0,2,1:T(8,128)}) fusion(f32[32,32,4]{0,2,1:T(4,128)S(1)} %copy.75, f32[96,32,4,48]{3,1,2,0:T(8,128)S(1)} %bitcast_multiply_fusion, s32[96]{0:T(128)S(1)} %copy-done.3), kind=kOutput, calls=%fused_computation.20 | convolution fusion | flops 226888704 | bytes 3555712 | tf_op jit(solution)/shard_map/nr,nqhs->rqhs/dot_general | solution.py:56
  41.1 0.5 copy.76
  41.7 0.6 reshape.213
  42.2 0.6 fusion.74
  42.9 0.7 fusion.73
  43.5 0.6 fusion.72
  44.2 0.7 fusion.71
  44.8 0.6 fusion.70
  45.5 0.7 fusion.69
  46.1 0.6 fusion.68
  46.8 0.7 fusion.67
  47.4 7.3 %all-to-all-start = ((bf16[8,32,4,192]{3,2,1,0:T(4,128)(2,1)}), bf16[8,32,4,192]{3,2,1,0:T(4,128)(2,1)S(1)}, u32[]{:S(2)}, u32[]{:S(2)}) async-start(bf16[8,32,4,192]{3,2,1,0:T(4,128)(2,1)} %fusion.67), calls=%async_computation | async-start | bytes 1048576 | tf_op jit(solution)/shard_map/all_to_all | solution.py:89
  54.7 0.2 reduce-scatter.2.cloned.1.call-start
  55.0 14.2 %all-to-all-done = bf16[8,32,4,192]{3,2,1,0:T(4,128)(2,1)S(1)} async-done(((bf16[8,32,4,192]{3,2,1,0:T(4,128)(2,1)}), bf16[8,32,4,192]{3,2,1,0:T(4,128)(2,1)S(1)}, u32[]{:S(2)}, u32[]{:S(2)}) %all-to-all-start) | async-done | bytes 393248 | tf_op jit(solution)/shard_map/all_to_all | solution.py:89
  69.2 0.1 convert_bitcast_fusion
  69.3 0.6 copy.80
  69.9 0.6 copy.79
  70.6 1.3 reshape.215
  71.8 0.5 reshape.216
  72.3 3.9 %fusion.34 = (f32[32,4]{0,1:T(4,128)S(1)}, f32[32,4,32,48]{3,0,1,2:T(8,128)S(1)}) fusion(f32[32,4,32,48]{3,2,1,0:T(8,128)S(1)} %reshape.216, f32[32,4,32]{0,1,2:T(4,128)S(1)} %copy.73, f32[32,32,4,48]{3,0,2,1:T(8,128)} %get-tuple-element.14), kind=kLoop, calls=%fused_computation.50 | loop fusion | flops 982912 | bytes 2376192 | tf_op jit(solution)/shard_map/reduce_sum | solution.py:63
  76.2 2.6 %copy.74 = f32[32,4,32,48]{3,2,0,1:T(8,128)} copy(f32[32,4,32,48]{3,0,1,2:T(8,128)S(1)} %get-tuple-element.8) | data formatting | bytes 1572864 | tf_op jit(solution)/shard_map/convert_element_type | solution.py:106
  78.8 1.4 multiply_reduce_fusion
  80.2 2.9 %reshape.214 = f32[32,4,1536]{2,0,1:T(8,128)S(1)} reshape(f32[32,4,32,48]{3,2,0,1:T(8,128)} %copy.74) | data formatting | bytes 1572864 | tf_op jit(solution)/shard_map/convert_element_type | solution.py:106
  83.2 0.2 multiply_convert_fusion.1
  83.4 10.4 %all_gather.3 = bf16[64,4,1536]{2,0,1:T(8,128)(2,1)S(1)} all-gather(bf16[32,4,1536]{2,0,1:T(8,128)(2,1)S(1)} %multiply_convert_fusion.1), channel_id=1, replica_groups=mesh['batch'=2,'token'=8,'hidden'=2] {'hidden'}, dimensions={0}, use_global_device_ids=true | all-gather | bytes 1179648 | tf_op jit(solution)/shard_map/all_gather | solution.py:110
  93.8 17.5 %convolution_bitcast_fusion = f32[64,4,1536]{2,0,1:T(8,128)} fusion(bf16[4,1536,1536]{2,1,0:T(8,128)(2,1)} %param.14, bf16[64,4,1536]{2,0,1:T(8,128)(2,1)S(1)} %all_gather.3, bf16[4,1536,1536]{2,1,0:T(8,128)(2,1)} %param.13), kind=kOutput, calls=%fused_computation.14 | convolution fusion | flops 2441478144 | bytes 40108032 | tf_op jit(solution)/shard_map/ntf,tfd->ntd/dot_general | solution.py:115
  111.3 26.9 %reduce-scatter.2.cloned.1.call-done = f32[32,4,1536]{2,0,1:T(8,128)} async-done(((f32[64,4,1536]{2,0,1:T(8,128)}), f32[32,4,1536]{2,0,1:T(8,128)}) %reduce-scatter.2.cloned.1.call-update) | async-done | bytes 786448 | tf_op jit(solution)/shard_map/reduce_scatter | solution.py:116
  138.2 1.4 fusion.66
  139.6 0.2 multiply_reduce_fusion.1
  139.8 0.2 multiply_convert_fusion
  140.0 1.1 copy.82
  (27 shorter events, 0.4 us)
Async XLA Ops:
  7.7 0.7 copy-start.2
  27.4 4.9 %copy-start.3 = (s32[96]{0:T(128)S(1)}, s32[96]{0:T(128)}, u32[]{:S(2)}) copy-start(s32[96]{0:T(128)} %copy-done.2) | copy-start | bytes 1156
  47.4 21.8 %all-to-all-start = ((bf16[8,32,4,192]{3,2,1,0:T(4,128)(2,1)}), bf16[8,32,4,192]{3,2,1,0:T(4,128)(2,1)S(1)}, u32[]{:S(2)}, u32[]{:S(2)}) async-start(bf16[8,32,4,192]{3,2,1,0:T(4,128)(2,1)} %fusion.67), calls=%async_computation | async-start | bytes 1048576 | tf_op jit(solution)/shard_map/all_to_all | solution.py:89
  54.7 83.5 %reduce-scatter.2.cloned.1.call-start = ((), (), s32[]{:S(2)}) async-start(), calls=%async_computation.2 | async-start | bytes 2359296 | tf_op jit(solution)/shard_map/reduce_scatter | solution.py:116
  80.2 2.9 %copy-start.1 = (f32[32,4,1536]{2,0,1:T(8,128)S(1)}, f32[32,4,1536]{2,0,1:T(8,128)}, u32[]{:S(2)}) copy-start(f32[32,4,1536]{2,0,1:T(8,128)} %reshape.215) | copy-start | bytes 2359300
  80.2 2.9 %copy-start.4 = (f32[1536]{0:T(1024)S(1)}, f32[1536]{0:T(1024)}, u32[]{:S(2)}) copy-start(f32[1536]{0:T(1024)} %param.12) | copy-start | bytes 18436
  111.3 28.5 %copy-start.5 = (f32[1536]{0:T(1024)S(1)}, f32[1536]{0:T(1024)}, u32[]{:S(2)}) copy-start(f32[1536]{0:T(1024)} %param.15) | copy-start | bytes 18436
  138.2 1.4 copy-start
Sparse Core Ops, SparseCore 0:
  111.4 26.7 reduce-scatter.1
